TPU v7x, 256 devices: a whole 4x4x8 slice. The times are simulated.
256 devices in a mesh: gx: 8 (over z), gy: 4 (over y), gz: 8 (over x, core).
Axes of the slice: x: 4, y: 4, z: 8, core: 2. Of those that a mesh axis runs over, the one named last changes fastest.
Arguments:
- signal: float32 [16, 1048576], P(None, ('gx', 'gy', 'gz')), may hold values from -6 to 6
- order: int32 [1048576], P(('gx', 'gy', 'gz')), may hold values from 0 to 4095, as said below
- near_tiles: bfloat16 [4096, 3, 256, 256], P(('gx', 'gy', 'gz')), may hold values from -0.21875 to 0.21875
- near_list: int32 [4096, 3], P(('gx', 'gy', 'gz')), may hold values from 0 to 4095, as said below
- leaf_basis: bfloat16 [4096, 64, 256], P(('gx', 'gy', 'gz')), may hold values from -0.375 to 0.375
- leaf_transfer: bfloat16 [4096, 64, 64], P(('gx', 'gy', 'gz')), may hold values from -0.5 to 0.5
- leaf_coupling: bfloat16 [4096, 64, 192], P(('gx', 'gy', 'gz')), may hold values from -0.4375 to 0.4375
- leaf_links: int32 [4096, 3], P(('gx', 'gy', 'gz')), may hold values from 0 to 4095, as said below
- device_transfer: bfloat16 [256, 64, 64], P(('gx', 'gy', 'gz')), may hold values from -0.5 to 0.5
- device_coupling: bfloat16 [256, 64, 192], P(('gx', 'gy', 'gz')), may hold values from -0.15625 to 0.15625
- device_links: int32 [256, 3], P(('gx', 'gy', 'gz')), may hold values from 0 to 255, as said below
- block_transfer: bfloat16 [32, 64, 64], P(('gx', 'gy')), may hold values from -0.5 to 0.5
- block_coupling: bfloat16 [32, 64, 192], P(('gx', 'gy')), may hold values from -0.078125 to 0.078125
- block_links: int32 [32, 3], P(('gx', 'gy')), may hold values from 0 to 31, as said below
- top_coupling: bfloat16 [8, 64, 192], P('gx'), may hold values from -0.0546875 to 0.0546875
- top_links: int32 [8, 3], P('gx'), may hold values from 0 to 7, as said below
Outputs:
- smoothed: float32 [16, 1048576], P(None, ('gx', 'gy', 'gz'))
- twice: float32 [16, 1048576], P(None, ('gx', 'gy', 'gz'))
Inputs may be any that keep to these rules, and one draw needn't show every extreme that they name: `order`: each device's block of 4096 consecutive entries is a permutation of 0 to 4095. `near_list`: row i holds i first, then two different leaves j with 1 <= |j - i| <= 2. `leaf_links`: row i holds three different leaves j with 2 <= |j - i| <= 4. `device_links`: row i holds three different device clusters j with 1 <= |j - i| <= 3. `block_links`: row i holds three different second-level clusters other than i. `top_links`: row i holds three different first-level clusters other than i.
All inputs are finite; a program needn't handle non-finite values.
Results may differ from a plain program's by a relative error of at most 0.0043.
Values may be sent and summed in bfloat16 or wider, within the bound.
A program may use at most 64 MiB of HBM per device.

v0:
```python
import jax
import jax.numpy as jnp
from jax import lax
from jax.sharding import PartitionSpec as P

NEAR_REACH = 2
LINK_REACH = 4
DEVICE_REACH = 3


HIGH = lax.Precision.HIGHEST


def shifted(block, axis, distance):
    devices = range(lax.axis_size(axis))
    route = [(i - distance, i) for i in devices if i - distance in devices]
    return lax.ppermute(block, axis, route)


def copy_for_each(x, axis):
    copies = jnp.broadcast_to(x, (lax.axis_size(axis), *x.shape))
    return lax.all_to_all(copies, axis, split_axis=0, concat_axis=0, tiled=True)


def taken_together(x, axis):
    return copy_for_each(x, axis).sum(axis=0)


def joined_along(blocks, dim):
    blocks = jnp.moveaxis(blocks, 0, dim)
    dims = blocks.shape
    return blocks.reshape(*dims[:dim], dims[dim] * dims[dim + 1], *dims[dim + 2 :])


def collect(x, axis, dim):
    blocks = copy_for_each(x, axis)
    return joined_along(blocks, dim)


def couple(picked, coupling):
    rank_dim = coupling.shape[0]
    link_count = picked.shape[0]
    table = coupling.astype(jnp.float32).reshape(rank_dim, link_count, rank_dim)
    return jnp.einsum("jrk,kjm->rm", picked, table, precision=HIGH)


def spread_down(parent, transfer):
    return jnp.dot(parent, transfer.astype(jnp.float32).T, precision=HIGH)


def relay_side(own_moment, direction):
    window = own_moment[None][:0]
    for step in range(DEVICE_REACH):
        outgoing = jnp.concatenate([own_moment[None], window], axis=0)
        window = shifted(outgoing, ("gx", "gy", "gz"), direction)
    return window


def apply_matrix(
    leaves,
    near_tiles,
    near_list,
    leaf_basis,
    leaf_transfer,
    leaf_coupling,
    leaf_links,
    device_transfer,
    device_coupling,
    device_links,
    block_transfer,
    block_coupling,
    block_links,
    top_coupling,
    top_links,
):
    leaf_dev = leaves.shape[1]
    device = lax.axis_index(("gx", "gy", "gz"))
    first_leaf = device * leaf_dev
    rims = []
    for offset, edge in ((1, leaves[:, leaf_dev - NEAR_REACH :]), (-1, leaves[:, :NEAR_REACH])):
        rims.append(shifted(edge, ("gx", "gy", "gz"), offset))
    widened = jnp.concatenate([rims[0], leaves, rims[1]], axis=1)
    moments = jnp.einsum("rls,lks->rlk", leaves, leaf_basis, preferred_element_type=jnp.float32)
    edges = []
    for offset, edge in ((1, moments[:, leaf_dev - LINK_REACH :]), (-1, moments[:, :LINK_REACH])):
        edges.append(shifted(edge, ("gx", "gy", "gz"), offset))
    wide_moments = jnp.concatenate([edges[0], moments, edges[1]], axis=1)
    transfer_f = leaf_transfer.astype(jnp.float32)
    own_moment = jnp.einsum("rlk,lkm->rm", moments, transfer_f, precision=HIGH)
    block_term = jnp.dot(own_moment, device_transfer[0].astype(jnp.float32), precision=HIGH)
    block_moment = taken_together(block_term, "gz")
    lower = relay_side(own_moment, 1)
    upper = relay_side(own_moment, -1)
    stacked = jnp.concatenate([lower[::-1], upper], axis=0)
    relative = device_links[0] - device
    position = relative + DEVICE_REACH - (relative > 0).astype(jnp.int32)
    device_picked = stacked[position]
    top_term = jnp.dot(block_moment, block_transfer[0].astype(jnp.float32), precision=HIGH)
    top_moment = taken_together(top_term, "gy")
    every_top = collect(top_moment[None], "gx", 0)
    every_block = collect(block_moment[None], ("gx", "gy"), 0)
    top_field = couple(every_top[top_links[0]], top_coupling[0])
    block_field = couple(every_block[block_links[0]], block_coupling[0]) + spread_down(
        top_field, block_transfer[0]
    )
    device_field = couple(device_picked, device_coupling[0]) + spread_down(
        block_field, device_transfer[0]
    )
    local_links = leaf_links - first_leaf + LINK_REACH
    picked = wide_moments[:, local_links]
    rank_dim = leaf_coupling.shape[1]
    leaf_table = leaf_coupling.astype(jnp.float32).reshape(leaf_dev, rank_dim, -1, rank_dim)
    leaf_field = jnp.einsum("rljk,lkjm->rlm", picked, leaf_table, precision=HIGH)
    leaf_field = leaf_field + jnp.einsum("rm,lkm->rlk", device_field, transfer_f, precision=HIGH)
    far_part = jnp.einsum(
        "rlk,lks->rls",
        leaf_field.astype(jnp.bfloat16),
        leaf_basis,
        preferred_element_type=jnp.float32,
    )
    near_index = near_list - first_leaf + NEAR_REACH
    near_rows = widened[:, near_index]
    near_part = jnp.einsum(
        "rlns,lnst->rlt", near_rows, near_tiles, preferred_element_type=jnp.float32
    )
    return near_part + far_part


def shards(
    signal,
    order,
    near_tiles,
    near_list,
    leaf_basis,
    leaf_transfer,
    leaf_coupling,
    leaf_links,
    device_transfer,
    device_coupling,
    device_links,
    block_transfer,
    block_coupling,
    block_links,
    top_coupling,
    top_links,
):
    matrices = (
        near_tiles,
        near_list,
        leaf_basis,
        leaf_transfer,
        leaf_coupling,
        leaf_links,
        device_transfer,
        device_coupling,
        device_links,
        block_transfer,
        block_coupling,
        block_links,
        top_coupling,
        top_links,
    )
    rhs_count = signal.shape[0]
    leaf_count = near_tiles.shape[0]
    tree = jnp.take(signal, order, axis=1).astype(jnp.bfloat16).reshape(rhs_count, leaf_count, -1)
    first = apply_matrix(tree, *matrices)
    second = apply_matrix(first.astype(jnp.bfloat16), *matrices)
    empty = jnp.zeros_like(signal)
    smoothed = empty.at[:, order].set(first.reshape(rhs_count, -1))
    twice = empty.at[:, order].set(second.reshape(rhs_count, -1))
    return (smoothed, twice)


def solution(mesh):
    in_specs = (
        P(None, ("gx", "gy", "gz")),
        P(("gx", "gy", "gz")),
        P(("gx", "gy", "gz"), None, None, None),
        P(("gx", "gy", "gz"), None),
        P(("gx", "gy", "gz"), None, None),
        P(("gx", "gy", "gz"), None, None),
        P(("gx", "gy", "gz"), None, None),
        P(("gx", "gy", "gz"), None),
        P(("gx", "gy", "gz"), None, None),
        P(("gx", "gy", "gz"), None, None),
        P(("gx", "gy", "gz"), None),
        P(("gx", "gy"), None, None),
        P(("gx", "gy"), None, None),
        P(("gx", "gy"), None),
        P("gx", None, None),
        P("gx", None),
    )
    out_specs = (P(None, ("gx", "gy", "gz")), P(None, ("gx", "gy", "gz")))
    return jax.shard_map(shards, mesh=mesh, in_specs=in_specs, out_specs=out_specs, check_vma=False)
```

profile of v0, /device:TPU:32, one launch (start us, length us, event | category | flops | bytes accessed | tf_op | source)
XLA Modules:
  0.0 242.1 jit_solution(4698943368862516332)
XLA Ops:
  4.4 12.1 %gather_fusion = bf16[4096,16]{1,0:T(8,128)(2,1)S(1)} fusion(bf16[16,4096]{0,1:T(8,128)(2,1)S(1)} %copy.38, s32[4096]{0:T(1024)S(1)} %get-tuple-element.16), kind=kCustom, calls=%fused_computation | custom fusion | bytes 278528 | tf_op jit(solution)/shard_map/jit(_take)/gather | solution.py:165
  17.4 6.1 %collective-permute-start.7 = (f32[1,16,64]{2,1,0:T(8,128)S(1)}, f32[1,16,64]{2,1,0:T(8,128)S(1)}, u32[]{:S(2)}, u32[]{:S(2)}) collective-permute-start(f32[1,16,64]{2,1,0:T(8,128)S(1)} %bitcast.191), channel_id=1, source_target_pairs={{1,0},{2,1},{3,2},{4,3},{5,4},{6,5},{7,6},{8,7},{9,8},{10,9},{11,1... | collective-permute-start | bytes 12296 | tf_op jit(solution)/shard_map/ppermute | solution.py:17
  27.4 7.9 %collective-permute-start.1 = (bf16[16,2,256]{2,0,1:T(8,128)(2,1)S(1)}, bf16[16,2,256]{2,0,1:T(8,128)(2,1)S(1)}, u32[]{:S(2)}, u32[]{:S(2)}) collective-permute-start(bf16[16,2,256]{2,0,1:T(8,128)(2,1)S(1)} %get-tuple-element.15), channel_id=1, source_target_pairs={{1,0},{2,1},{3,2},{4,3},{5,4},{6,5},{7,6},{8,7},{9,8},{10,9},{11,1... | collective-permute-start | bytes 49160 | tf_op jit(solution)/shard_map/ppermute | solution.py:17
  36.1 3.3 %all-to-all-start = ((f32[8,1,1024]{2,1,0:T(1,128)}), f32[8,1,1024]{2,1,0:T(1,128)S(1)}, u32[]{:S(2)}, u32[]{:S(2)}) async-start(f32[8,1,1024]{2,1,0:T(1,128)} %reshape.291), calls=%async_computation | async-start | bytes 65536 | tf_op jit(solution)/shard_map/all_to_all | solution.py:22
  39.5 2.3 collective-permute-start.2
  42.4 3.5 %collective-permute-start.5 = (f32[2,16,64]{2,1,0:T(8,128)S(1)}, f32[2,16,64]{2,1,0:T(8,128)S(1)}, u32[]{:S(2)}, u32[]{:S(2)}) collective-permute-start(f32[2,16,64]{2,1,0:T(8,128)S(1)} %get-tuple-element.24), channel_id=1, source_target_pairs={{0,1},{1,2},{2,3},{3,4},{4,5},{5,6},{6,7},{7,8},{8,9},{9,10},{10,1... | collective-permute-start | bytes 24584 | tf_op jit(solution)/shard_map/ppermute | solution.py:17
  46.0 6.2 %collective-permute-start.8 = (f32[2,16,64]{2,1,0:T(8,128)S(1)}, f32[2,16,64]{2,1,0:T(8,128)S(1)}, u32[]{:S(2)}, u32[]{:S(2)}) collective-permute-start(f32[2,16,64]{2,1,0:T(8,128)S(1)} %get-tuple-element.25), channel_id=1, source_target_pairs={{1,0},{2,1},{3,2},{4,3},{5,4},{6,5},{7,6},{8,7},{9,8},{10,9},{11,1... | collective-permute-start | bytes 24584 | tf_op jit(solution)/shard_map/ppermute | solution.py:17
  53.0 2.0 collective-permute-start.3
  55.1 2.3 collective-permute-start.6
  59.5 3.3 %all-to-all-start.2 = ((f32[4,1,1024]{2,1,0:T(1,128)}), f32[4,1,1024]{2,1,0:T(1,128)S(1)}, u32[]{:S(2)}, u32[]{:S(2)}) async-start(f32[4,1,1024]{2,1,0:T(1,128)} %reshape.295), calls=%async_computation.2 | async-start | bytes 32768 | tf_op jit(solution)/shard_map/all_to_all | solution.py:22
  62.8 8.1 %collective-permute-start.9 = (f32[3,16,64]{2,1,0:T(8,128)S(1)}, f32[3,16,64]{2,1,0:T(8,128)S(1)}, u32[]{:S(2)}, u32[]{:S(2)}) collective-permute-start(f32[3,16,64]{2,1,0:T(8,128)S(1)} %get-tuple-element.23), channel_id=1, source_target_pairs={{1,0},{2,1},{3,2},{4,3},{5,4},{6,5},{7,6},{8,7},{9,8},{10,9},{11,1... | collective-permute-start | bytes 36872 | tf_op jit(solution)/shard_map/ppermute | solution.py:17
  73.0 12.2 %all-to-all-start.3 = ((f32[8,1,1024]{2,1,0:T(1,128)}), f32[8,1,1024]{2,1,0:T(1,128)S(1)}, u32[]{:S(2)}, u32[]{:S(2)}) async-start(f32[8,1,1024]{2,1,0:T(1,128)} %reshape.297), calls=%async_computation.3 | async-start | bytes 65536 | tf_op jit(solution)/shard_map/all_to_all | solution.py:22
  85.2 3.7 %convolution_bitcast_fusion.1 = f32[16,16,256]{2,1,0:T(8,128)S(1)} fusion(bf16[16,16,3,256]{3,0,2,1:T(8,128)(2,1)S(1)} %bitcast.176, bf16[16,3,256,256]{3,2,1,0:T(8,128)(2,1)} %param.18), kind=kOutput, calls=%fused_computation.17 | convolution fusion | flops 100663296 | bytes 6946816 | tf_op jit(solution)/shard_map/rlns,lnst->rlt/dot_general | solution.py:123
  89.8 2.0 all-to-all-done.3
  91.8 5.4 %all-to-all-start.1 = ((f32[32,1,1024]{2,1,0:T(1,128)}), f32[32,1,1024]{2,1,0:T(1,128)S(1)}, u32[]{:S(2)}, u32[]{:S(2)}) async-start(f32[32,1,1024]{2,1,0:T(1,128)} %reshape.293), calls=%async_computation.1 | async-start | bytes 262144 | tf_op jit(solution)/shard_map/all_to_all | solution.py:22
  99.9 6.8 %all-to-all-done.1 = f32[32,1,1024]{2,1,0:T(1,128)S(1)} async-done(((f32[32,1,1024]{2,1,0:T(1,128)}), f32[32,1,1024]{2,1,0:T(1,128)S(1)}, u32[]{:S(2)}, u32[]{:S(2)}) %all-to-all-start.1) | async-done | bytes 131104 | tf_op jit(solution)/shard_map/all_to_all | solution.py:22
  113.3 2.4 collective-permute-start.14
  116.9 5.5 %collective-permute-done.14 = f32[1,16,64]{2,1,0:T(8,128)S(1)} collective-permute-done((f32[1,16,64]{2,1,0:T(8,128)S(1)}, f32[1,16,64]{2,1,0:T(8,128)S(1)}, u32[]{:S(2)}, u32[]{:S(2)}) %collective-permute-start.14) | collective-permute-done | bytes 4128 | tf_op jit(solution)/shard_map/ppermute | solution.py:17
  125.0 7.9 %collective-permute-start.18 = (f32[2,16,64]{2,1,0:T(8,128)}, f32[2,16,64]{2,1,0:T(8,128)}, u32[]{:S(2)}, u32[]{:S(2)}) collective-permute-start(f32[2,16,64]{2,1,0:T(8,128)} %get-tuple-element.21), channel_id=1, source_target_pairs={{1,0},{2,1},{3,2},{4,3},{5,4},{6,5},{7,6},{8,7},{9,8},{10,9},{11,1... | collective-permute-start | bytes 24584 | tf_op jit(solution)/shard_map/ppermute | solution.py:17
  134.9 7.9 %collective-permute-start.11 = (bf16[16,2,256]{2,0,1:T(8,128)(2,1)}, bf16[16,2,256]{2,0,1:T(8,128)(2,1)}, u32[]{:S(2)}, u32[]{:S(2)}) collective-permute-start(bf16[16,2,256]{2,0,1:T(8,128)(2,1)} %get-tuple-element.11), channel_id=1, source_target_pairs={{1,0},{2,1},{3,2},{4,3},{5,4},{6,5},{7,6},{8,7},{9,8},{10,9},{11,1... | collective-permute-start | bytes 49160 | tf_op jit(solution)/shard_map/ppermute | solution.py:17
  143.5 3.9 %all-to-all-start.4 = ((f32[8,1,1024]{2,1,0:T(1,128)}), f32[8,1,1024]{2,1,0:T(1,128)}, u32[]{:S(2)}, u32[]{:S(2)}) async-start(f32[8,1,1024]{2,1,0:T(1,128)} %reshape.299), calls=%async_computation.4 | async-start | bytes 65536 | tf_op jit(solution)/shard_map/all_to_all | solution.py:22
  147.5 2.3 collective-permute-start.12
  149.7 2.0 copy.51
  151.7 11.4 %scatter_custom_fusion = f32[16,4096]{0,1:T(8,128)S(1)} fusion(s32[4096]{0:T(1024)} %get-tuple-element.17, f32[4096,16]{1,0:T(8,128)} %copy.51, f32[]{:T(128)} %constant.17.clone.1), kind=kCustom, calls=%fused_computation.40 | custom fusion | bytes 262656 | tf_op jit(solution)/shard_map/scatter | solution.py:169
  164.4 7.5 %collective-permute-start.13 = (f32[16,4,64]{2,0,1:T(8,128)}, f32[16,4,64]{2,0,1:T(8,128)S(1)}, u32[]{:S(2)}, u32[]{:S(2)}) collective-permute-start(f32[16,4,64]{2,0,1:T(8,128)} %get-tuple-element.9), channel_id=1, source_target_pairs={{1,0},{2,1},{3,2},{4,3},{5,4},{6,5},{7,6},{8,7},{9,8},{10,9},{11,1... | collective-permute-start | bytes 49160 | tf_op jit(solution)/shard_map/ppermute | solution.py:17
  176.9 3.2 %all-to-all-start.6 = ((f32[4,1,1024]{2,1,0:T(1,128)}), f32[4,1,1024]{2,1,0:T(1,128)S(1)}, u32[]{:S(2)}, u32[]{:S(2)}) async-start(f32[4,1,1024]{2,1,0:T(1,128)} %reshape.303), calls=%async_computation.6 | async-start | bytes 32768 | tf_op jit(solution)/shard_map/all_to_all | solution.py:22
  180.2 8.5 %collective-permute-start.19 = (f32[3,16,64]{2,1,0:T(8,128)S(1)}, f32[3,16,64]{2,1,0:T(8,128)S(1)}, u32[]{:S(2)}, u32[]{:S(2)}) collective-permute-start(f32[3,16,64]{2,1,0:T(8,128)S(1)} %get-tuple-element.19), channel_id=1, source_target_pairs={{1,0},{2,1},{3,2},{4,3},{5,4},{6,5},{7,6},{8,7},{9,8},{10,9},{11,1... | collective-permute-start | bytes 36872 | tf_op jit(solution)/shard_map/ppermute | solution.py:17
  191.9 9.6 %all-to-all-start.7 = ((f32[8,1,1024]{2,1,0:T(1,128)}), f32[8,1,1024]{2,1,0:T(1,128)S(1)}, u32[]{:S(2)}, u32[]{:S(2)}) async-start(f32[8,1,1024]{2,1,0:T(1,128)} %reshape.305), calls=%async_computation.7 | async-start | bytes 65536 | tf_op jit(solution)/shard_map/all_to_all | solution.py:22
  201.5 3.7 %convolution_bitcast_fusion = f32[16,16,256]{2,1,0:T(8,128)S(1)} fusion(bf16[16,16,3,256]{3,0,2,1:T(8,128)(2,1)S(1)} %bitcast.175, bf16[16,3,256,256]{3,2,1,0:T(8,128)(2,1)} %param.18), kind=kOutput, calls=%fused_computation.15 | convolution fusion | flops 100663296 | bytes 6946816 | tf_op jit(solution)/shard_map/rlns,lnst->rlt/dot_general | solution.py:123
  208.0 5.6 %all-to-all-start.5 = ((f32[32,1,1024]{2,1,0:T(1,128)}), f32[32,1,1024]{2,1,0:T(1,128)S(1)}, u32[]{:S(2)}, u32[]{:S(2)}) async-start(f32[32,1,1024]{2,1,0:T(1,128)} %reshape.301), calls=%async_computation.5 | async-start | bytes 262144 | tf_op jit(solution)/shard_map/all_to_all | solution.py:22
  217.4 5.8 %all-to-all-done.5 = f32[32,1,1024]{2,1,0:T(1,128)S(1)} async-done(((f32[32,1,1024]{2,1,0:T(1,128)}), f32[32,1,1024]{2,1,0:T(1,128)S(1)}, u32[]{:S(2)}, u32[]{:S(2)}) %all-to-all-start.5) | async-done | bytes 131104 | tf_op jit(solution)/shard_map/all_to_all | solution.py:22
  229.4 11.4 %scatter_custom_fusion.1 = f32[16,4096]{0,1:T(8,128)S(1)} fusion(s32[4096]{0:T(1024)} %get-tuple-element.17, f32[4096,16]{1,0:T(8,128)} %copy.57, f32[]{:T(128)} %constant.17.clone.1), kind=kCustom, calls=%fused_computation.38 | custom fusion | bytes 262656 | tf_op jit(solution)/shard_map/scatter | solution.py:170
  (205 shorter events, 54.2 us)
Async XLA Ops:
  17.4 25.0 %collective-permute-start.7 = (f32[1,16,64]{2,1,0:T(8,128)S(1)}, f32[1,16,64]{2,1,0:T(8,128)S(1)}, u32[]{:S(2)}, u32[]{:S(2)}) collective-permute-start(f32[1,16,64]{2,1,0:T(8,128)S(1)} %bitcast.191), channel_id=1, source_target_pairs={{1,0},{2,1},{3,2},{4,3},{5,4},{6,5},{7,6},{8,7},{9,8},{10,9},{11,1... | collective-permute-start | bytes 12296 | tf_op jit(solution)/shard_map/ppermute | solution.py:17
  23.5 18.9 %collective-permute-start.4 = (f32[1,16,64]{2,1,0:T(8,128)S(1)}, f32[1,16,64]{2,1,0:T(8,128)S(1)}, u32[]{:S(2)}, u32[]{:S(2)}) collective-permute-start(f32[1,16,64]{2,1,0:T(8,128)S(1)} %bitcast.192), channel_id=1, source_target_pairs={{0,1},{1,2},{2,3},{3,4},{4,5},{5,6},{6,7},{7,8},{8,9},{9,10},{10,1... | collective-permute-start | bytes 12296 | tf_op jit(solution)/shard_map/ppermute | solution.py:17
  25.5 37.3 %collective-permute-start = (bf16[16,2,256]{2,0,1:T(8,128)(2,1)S(1)}, bf16[16,2,256]{2,0,1:T(8,128)(2,1)S(1)}, u32[]{:S(2)}, u32[]{:S(2)}) collective-permute-start(bf16[16,2,256]{2,0,1:T(8,128)(2,1)S(1)} %get-tuple-element.14), channel_id=1, source_target_pairs={{0,1},{1,2},{2,3},{3,4},{4,5},{5,6},{6,7},{7,8},{8,9},{9,10},{10,1... | collective-permute-start | bytes 49160 | tf_op jit(solution)/shard_map/ppermute | solution.py:17
  27.4 43.5 %collective-permute-start.1 = (bf16[16,2,256]{2,0,1:T(8,128)(2,1)S(1)}, bf16[16,2,256]{2,0,1:T(8,128)(2,1)S(1)}, u32[]{:S(2)}, u32[]{:S(2)}) collective-permute-start(bf16[16,2,256]{2,0,1:T(8,128)(2,1)S(1)} %get-tuple-element.15), channel_id=1, source_target_pairs={{1,0},{2,1},{3,2},{4,3},{5,4},{6,5},{7,6},{8,7},{9,8},{10,9},{11,1... | collective-permute-start | bytes 49160 | tf_op jit(solution)/shard_map/ppermute | solution.py:17
  36.1 21.3 %all-to-all-start = ((f32[8,1,1024]{2,1,0:T(1,128)}), f32[8,1,1024]{2,1,0:T(1,128)S(1)}, u32[]{:S(2)}, u32[]{:S(2)}) async-start(f32[8,1,1024]{2,1,0:T(1,128)} %reshape.291), calls=%async_computation | async-start | bytes 65536 | tf_op jit(solution)/shard_map/all_to_all | solution.py:22
  39.5 57.7 %collective-permute-start.2 = (f32[16,4,64]{2,0,1:T(8,128)S(1)}, f32[16,4,64]{2,0,1:T(8,128)S(1)}, u32[]{:S(2)}, u32[]{:S(2)}) collective-permute-start(f32[16,4,64]{2,0,1:T(8,128)S(1)} %get-tuple-element.12), channel_id=1, source_target_pairs={{0,1},{1,2},{2,3},{3,4},{4,5},{5,6},{6,7},{7,8},{8,9},{9,10},{10,1... | collective-permute-start | bytes 49160 | tf_op jit(solution)/shard_map/ppermute | solution.py:17
  41.9 57.3 %copy-start.23 = (s32[1024]{0:T(1024)}, s32[1024]{0:T(1024)S(1)}, u32[]{:S(2)}) copy-start(s32[1024]{0:T(1024)S(1)} %pad_clamp_fusion) | copy-start | bytes 12292
  41.9 65.8 %copy-start.22 = (s32[1024]{0:T(1024)}, s32[1024]{0:T(1024)S(1)}, u32[]{:S(2)}) copy-start(s32[1024]{0:T(1024)S(1)} %pad_clamp_fusion.1) | copy-start | bytes 12292
  42.0 55.9 %copy-start.24 = (s32[1024]{0:T(1024)}, s32[1024]{0:T(1024)S(1)}, u32[]{:S(2)}) copy-start(s32[1024]{0:T(1024)S(1)} %pad_clamp_fusion.2) | copy-start | bytes 12292
  42.4 10.6 %collective-permute-start.5 = (f32[2,16,64]{2,1,0:T(8,128)S(1)}, f32[2,16,64]{2,1,0:T(8,128)S(1)}, u32[]{:S(2)}, u32[]{:S(2)}) collective-permute-start(f32[2,16,64]{2,1,0:T(8,128)S(1)} %get-tuple-element.24), channel_id=1, source_target_pairs={{0,1},{1,2},{2,3},{3,4},{4,5},{5,6},{6,7},{7,8},{8,9},{9,10},{10,1... | collective-permute-start | bytes 24584 | tf_op jit(solution)/shard_map/ppermute | solution.py:17
  46.0 9.1 %collective-permute-start.8 = (f32[2,16,64]{2,1,0:T(8,128)S(1)}, f32[2,16,64]{2,1,0:T(8,128)S(1)}, u32[]{:S(2)}, u32[]{:S(2)}) collective-permute-start(f32[2,16,64]{2,1,0:T(8,128)S(1)} %get-tuple-element.25), channel_id=1, source_target_pairs={{1,0},{2,1},{3,2},{4,3},{5,4},{6,5},{7,6},{8,7},{9,8},{10,9},{11,1... | collective-permute-start | bytes 24584 | tf_op jit(solution)/shard_map/ppermute | solution.py:17
  52.4 56.3 %copy-start.9 = (bf16[1,64,192]{1,2,0:T(8,128)(2,1)}, bf16[1,64,192]{1,2,0:T(8,128)(2,1)S(1)}, u32[]{:S(2)}) copy-start(bf16[1,64,192]{1,2,0:T(8,128)(2,1)S(1)} %copy.44) | copy-start | bytes 73732
  53.0 44.1 %collective-permute-start.3 = (f32[16,4,64]{2,0,1:T(8,128)S(1)}, f32[16,4,64]{2,0,1:T(8,128)S(1)}, u32[]{:S(2)}, u32[]{:S(2)}) collective-permute-start(f32[16,4,64]{2,0,1:T(8,128)S(1)} %get-tuple-element.13), channel_id=1, source_target_pairs={{1,0},{2,1},{3,2},{4,3},{5,4},{6,5},{7,6},{8,7},{9,8},{10,9},{11,1... | collective-permute-start | bytes 49160 | tf_op jit(solution)/shard_map/ppermute | solution.py:17
  55.1 42.7 %collective-permute-start.6 = (f32[3,16,64]{2,1,0:T(8,128)S(1)}, f32[3,16,64]{2,1,0:T(8,128)S(1)}, u32[]{:S(2)}, u32[]{:S(2)}) collective-permute-start(f32[3,16,64]{2,1,0:T(8,128)S(1)} %get-tuple-element.22), channel_id=1, source_target_pairs={{0,1},{1,2},{2,3},{3,4},{4,5},{5,6},{6,7},{7,8},{8,9},{9,10},{10,1... | collective-permute-start | bytes 36872 | tf_op jit(solution)/shard_map/ppermute | solution.py:17
  59.5 12.1 %all-to-all-start.2 = ((f32[4,1,1024]{2,1,0:T(1,128)}), f32[4,1,1024]{2,1,0:T(1,128)S(1)}, u32[]{:S(2)}, u32[]{:S(2)}) async-start(f32[4,1,1024]{2,1,0:T(1,128)} %reshape.295), calls=%async_computation.2 | async-start | bytes 32768 | tf_op jit(solution)/shard_map/all_to_all | solution.py:22
  62.8 35.1 %collective-permute-start.9 = (f32[3,16,64]{2,1,0:T(8,128)S(1)}, f32[3,16,64]{2,1,0:T(8,128)S(1)}, u32[]{:S(2)}, u32[]{:S(2)}) collective-permute-start(f32[3,16,64]{2,1,0:T(8,128)S(1)} %get-tuple-element.23), channel_id=1, source_target_pairs={{1,0},{2,1},{3,2},{4,3},{5,4},{6,5},{7,6},{8,7},{9,8},{10,9},{11,1... | collective-permute-start | bytes 36872 | tf_op jit(solution)/shard_map/ppermute | solution.py:17
  73.0 18.8 %all-to-all-start.3 = ((f32[8,1,1024]{2,1,0:T(1,128)}), f32[8,1,1024]{2,1,0:T(1,128)S(1)}, u32[]{:S(2)}, u32[]{:S(2)}) async-start(f32[8,1,1024]{2,1,0:T(1,128)} %reshape.297), calls=%async_computation.3 | async-start | bytes 65536 | tf_op jit(solution)/shard_map/all_to_all | solution.py:22
  91.8 14.9 %all-to-all-start.1 = ((f32[32,1,1024]{2,1,0:T(1,128)}), f32[32,1,1024]{2,1,0:T(1,128)S(1)}, u32[]{:S(2)}, u32[]{:S(2)}) async-start(f32[32,1,1024]{2,1,0:T(1,128)} %reshape.293), calls=%async_computation.1 | async-start | bytes 262144 | tf_op jit(solution)/shard_map/all_to_all | solution.py:22
  111.3 5.6 %collective-permute-start.17 = (f32[1,16,64]{2,1,0:T(8,128)S(1)}, f32[1,16,64]{2,1,0:T(8,128)S(1)}, u32[]{:S(2)}, u32[]{:S(2)}) collective-permute-start(f32[1,16,64]{2,1,0:T(8,128)S(1)} %bitcast.195), channel_id=1, source_target_pairs={{1,0},{2,1},{3,2},{4,3},{5,4},{6,5},{7,6},{8,7},{9,8},{10,9},{11,1... | collective-permute-start | bytes 12296 | tf_op jit(solution)/shard_map/ppermute | solution.py:17
  113.3 9.2 %collective-permute-start.14 = (f32[1,16,64]{2,1,0:T(8,128)S(1)}, f32[1,16,64]{2,1,0:T(8,128)S(1)}, u32[]{:S(2)}, u32[]{:S(2)}) collective-permute-start(f32[1,16,64]{2,1,0:T(8,128)S(1)} %bitcast.196), channel_id=1, source_target_pairs={{0,1},{1,2},{2,3},{3,4},{4,5},{5,6},{6,7},{7,8},{8,9},{9,10},{10,1... | collective-permute-start | bytes 12296 | tf_op jit(solution)/shard_map/ppermute | solution.py:17
  123.1 41.4 %collective-permute-start.15 = (f32[2,16,64]{2,1,0:T(8,128)}, f32[2,16,64]{2,1,0:T(8,128)}, u32[]{:S(2)}, u32[]{:S(2)}) collective-permute-start(f32[2,16,64]{2,1,0:T(8,128)} %get-tuple-element.20), channel_id=1, source_target_pairs={{0,1},{1,2},{2,3},{3,4},{4,5},{5,6},{6,7},{7,8},{8,9},{9,10},{10,1... | collective-permute-start | bytes 24584 | tf_op jit(solution)/shard_map/ppermute | solution.py:17
  125.0 47.0 %collective-permute-start.18 = (f32[2,16,64]{2,1,0:T(8,128)}, f32[2,16,64]{2,1,0:T(8,128)}, u32[]{:S(2)}, u32[]{:S(2)}) collective-permute-start(f32[2,16,64]{2,1,0:T(8,128)} %get-tuple-element.21), channel_id=1, source_target_pairs={{1,0},{2,1},{3,2},{4,3},{5,4},{6,5},{7,6},{8,7},{9,8},{10,9},{11,1... | collective-permute-start | bytes 24584 | tf_op jit(solution)/shard_map/ppermute | solution.py:17
  133.0 47.2 %collective-permute-start.10 = (bf16[16,2,256]{2,0,1:T(8,128)(2,1)}, bf16[16,2,256]{2,0,1:T(8,128)(2,1)}, u32[]{:S(2)}, u32[]{:S(2)}) collective-permute-start(bf16[16,2,256]{2,0,1:T(8,128)(2,1)} %get-tuple-element.10), channel_id=1, source_target_pairs={{0,1},{1,2},{2,3},{3,4},{4,5},{5,6},{6,7},{7,8},{8,9},{9,10},{10,1... | collective-permute-start | bytes 49160 | tf_op jit(solution)/shard_map/ppermute | solution.py:17
  134.9 53.8 %collective-permute-start.11 = (bf16[16,2,256]{2,0,1:T(8,128)(2,1)}, bf16[16,2,256]{2,0,1:T(8,128)(2,1)}, u32[]{:S(2)}, u32[]{:S(2)}) collective-permute-start(bf16[16,2,256]{2,0,1:T(8,128)(2,1)} %get-tuple-element.11), channel_id=1, source_target_pairs={{1,0},{2,1},{3,2},{4,3},{5,4},{6,5},{7,6},{8,7},{9,8},{10,9},{11,1... | collective-permute-start | bytes 49160 | tf_op jit(solution)/shard_map/ppermute | solution.py:17
  143.5 31.1 %all-to-all-start.4 = ((f32[8,1,1024]{2,1,0:T(1,128)}), f32[8,1,1024]{2,1,0:T(1,128)}, u32[]{:S(2)}, u32[]{:S(2)}) async-start(f32[8,1,1024]{2,1,0:T(1,128)} %reshape.299), calls=%async_computation.4 | async-start | bytes 65536 | tf_op jit(solution)/shard_map/all_to_all | solution.py:22
  147.5 66.2 %collective-permute-start.12 = (f32[16,4,64]{2,0,1:T(8,128)}, f32[16,4,64]{2,0,1:T(8,128)}, u32[]{:S(2)}, u32[]{:S(2)}) collective-permute-start(f32[16,4,64]{2,0,1:T(8,128)} %get-tuple-element.8), channel_id=1, source_target_pairs={{0,1},{1,2},{2,3},{3,4},{4,5},{5,6},{6,7},{7,8},{8,9},{9,10},{10,1... | collective-permute-start | bytes 49160 | tf_op jit(solution)/shard_map/ppermute | solution.py:17
  164.4 49.2 %collective-permute-start.13 = (f32[16,4,64]{2,0,1:T(8,128)}, f32[16,4,64]{2,0,1:T(8,128)S(1)}, u32[]{:S(2)}, u32[]{:S(2)}) collective-permute-start(f32[16,4,64]{2,0,1:T(8,128)} %get-tuple-element.9), channel_id=1, source_target_pairs={{1,0},{2,1},{3,2},{4,3},{5,4},{6,5},{7,6},{8,7},{9,8},{10,9},{11,1... | collective-permute-start | bytes 49160 | tf_op jit(solution)/shard_map/ppermute | solution.py:17
  172.7 42.4 %collective-permute-start.16 = (f32[3,16,64]{2,1,0:T(8,128)S(1)}, f32[3,16,64]{2,1,0:T(8,128)S(1)}, u32[]{:S(2)}, u32[]{:S(2)}) collective-permute-start(f32[3,16,64]{2,1,0:T(8,128)S(1)} %get-tuple-element.18), channel_id=1, source_target_pairs={{0,1},{1,2},{2,3},{3,4},{4,5},{5,6},{6,7},{7,8},{8,9},{9,10},{10,1... | collective-permute-start | bytes 36872 | tf_op jit(solution)/shard_map/ppermute | solution.py:17
  176.9 13.5 %all-to-all-start.6 = ((f32[4,1,1024]{2,1,0:T(1,128)}), f32[4,1,1024]{2,1,0:T(1,128)S(1)}, u32[]{:S(2)}, u32[]{:S(2)}) async-start(f32[4,1,1024]{2,1,0:T(1,128)} %reshape.303), calls=%async_computation.6 | async-start | bytes 32768 | tf_op jit(solution)/shard_map/all_to_all | solution.py:22
  180.2 34.9 %collective-permute-start.19 = (f32[3,16,64]{2,1,0:T(8,128)S(1)}, f32[3,16,64]{2,1,0:T(8,128)S(1)}, u32[]{:S(2)}, u32[]{:S(2)}) collective-permute-start(f32[3,16,64]{2,1,0:T(8,128)S(1)} %get-tuple-element.19), channel_id=1, source_target_pairs={{1,0},{2,1},{3,2},{4,3},{5,4},{6,5},{7,6},{8,7},{9,8},{10,9},{11,1... | collective-permute-start | bytes 36872 | tf_op jit(solution)/shard_map/ppermute | solution.py:17
  191.9 16.2 %all-to-all-start.7 = ((f32[8,1,1024]{2,1,0:T(1,128)}), f32[8,1,1024]{2,1,0:T(1,128)S(1)}, u32[]{:S(2)}, u32[]{:S(2)}) async-start(f32[8,1,1024]{2,1,0:T(1,128)} %reshape.305), calls=%async_computation.7 | async-start | bytes 65536 | tf_op jit(solution)/shard_map/all_to_all | solution.py:22
  208.0 15.2 %all-to-all-start.5 = ((f32[32,1,1024]{2,1,0:T(1,128)}), f32[32,1,1024]{2,1,0:T(1,128)S(1)}, u32[]{:S(2)}, u32[]{:S(2)}) async-start(f32[32,1,1024]{2,1,0:T(1,128)} %reshape.301), calls=%async_computation.5 | async-start | bytes 262144 | tf_op jit(solution)/shard_map/all_to_all | solution.py:22
  (26 other events, 857.0 us)
where the time goes:
time: 244 us; the launch traced here: 242 us
  starting transfers between devices  133 us (55%)
  local copies, waits for them, and re-layouts  59.1 us (24%)
  waiting for transfers between devices  22.2 us (9%)
  matrix products  14.2 us (6%)
  other arithmetic  11.7 us (5%)
    ppermute x20, starting transfers between devices, shifted(): return lax.ppermute(block, axis, route)  86.5 us
    all_to_all x8, starting transfers between devices, copy_for_each(): return lax.all_to_all(copies, axis, split_axis=0, concat_axis=0, tiled=True)  46.5 us
    all_to_all x8, waiting for transfers between devices, copy_for_each(): return lax.all_to_all(copies, axis, split_axis=0, concat_axis=0, tiled=True)  16.6 us
    gather x2, local copies, waits for them, and re-layouts, shards(): jnp.take(signal, order, axis=1).astype(jnp.bfloat16)  12.4 us
    unnamed x83, local copies, waits for them, and re-layouts  11.5 us
    scatter x1, local copies, waits for them, and re-layouts, shards(): smoothed = empty.at[:, order].set(first.reshape(rhs_count, -1))  11.4 us
    scatter x1, local copies, waits for them, and re-layouts, shards(): twice = empty.at[:, order].set(second.reshape(rhs_count, -1))  11.4 us
    dot_general x2, matrix products, apply_matrix(): jnp.einsum('rlns,lnst->rlt', near_rows, near_tiles, preferred_element_typ...  7.41 us
  transfers between devices with their start and end apart: 28, of which 5 were waited for; matrix products, arithmetic and copies ran while one was open for 18% of the time, Pallas kernels for 0%

commit v1 on v0

v1 whole, which is shorter than its diff:
```python
import functools

import jax
import jax.numpy as jnp
from jax import lax
from jax.experimental import pallas as pl
from jax.experimental.pallas import tpu as pltpu
from jax.sharding import PartitionSpec as P

MESH = pl.DeviceIdType.MESH
NEAR_REACH = 2
LINK_REACH = 4
DEVICE_REACH = 3
LINKS = 3
F32 = jnp.float32
BF16 = jnp.bfloat16


def nn(a, b):
    return lax.dot_general(a, b, (((1,), (0,)), ((), ())), preferred_element_type=F32)


def nt(a, b):
    return lax.dot_general(a, b, (((1,), (1,)), ((), ())), preferred_element_type=F32)


def within(index, ref):
    return jnp.minimum(jnp.maximum(index, 0), ref.shape[0] - 1)


def halves(x):
    top = x.astype(BF16)
    return jnp.concatenate([top, (x - top.astype(F32)).astype(BF16)], axis=0)


def fine(product, x, weights):
    both = product(halves(x), weights)
    return both[: x.shape[0]] + both[x.shape[0] :]


def parts_of(x):
    top = x.astype(BF16)
    return top, (x - top.astype(F32)).astype(BF16)


def full(x, tops, rests):
    both = nn(halves(x), tops)
    return both[: x.shape[0]] + both[x.shape[0] :] + nn(x.astype(BF16), rests)


def placed(rows, cols, offset):
    i = lax.broadcasted_iota(jnp.int32, (rows, cols), 0)
    j = lax.broadcasted_iota(jnp.int32, (rows, cols), 1)
    return jnp.where(j == i + offset, 1.0, 0.0).astype(F32)


def kernel(
    n_gx,
    n_gy,
    n_gz,
    near_list,
    leaf_links,
    device_links,
    block_links,
    top_links,
    signal,
    order,
    near_tiles,
    leaf_basis,
    leaf_transfer,
    leaf_coupling,
    device_transfer,
    device_coupling,
    block_transfer,
    block_coupling,
    top_coupling,
    smoothed,
    twice,
    sig_v,
    ord_v,
    tiles_v,
    basis_v,
    lt_v,
    lc_v,
    dt_v,
    dc_v,
    bt_v,
    bc_v,
    tc_v,
    hot_v,
    scat_v,
    vw_0,
    vw_1,
    mw_0,
    mw_1,
    raw_0,
    raw_1,
    r1_src,
    r1_buf,
    r2_0,
    r2_1,
    near_v,
    coup_v,
    qt_v,
    mix_v,
    local_sem,
    halo_send,
    halo_recv,
    raw_send,
    raw_recv,
    r1_send,
    r1_recv,
    r2_send,
    r2_recv,
):
    rhs, points = sig_v.shape
    leaves, rank, leaf = basis_v.shape
    slabs = points // leaf
    n_blocks = n_gx * n_gy
    n_devices = n_blocks * n_gz
    gx, gy, gz = lax.axis_index("gx"), lax.axis_index("gy"), lax.axis_index("gz")
    block = gx * n_gy + gy
    device = block * n_gz + gz
    first_leaf = device * leaves

    def mesh_id(index):
        index = lax.rem(index + n_devices, n_devices)
        row = index // n_gz
        return {"gx": row // n_gy, "gy": lax.rem(row, n_gy), "gz": lax.rem(index, n_gz)}

    def plane_id(k):
        other = lax.rem(block + k, n_blocks)
        return {"gx": other // n_gy, "gy": lax.rem(other, n_gy), "gz": gz}

    def line_id(k):
        return {"gx": gx, "gy": gy, "gz": lax.rem(gz + k, n_gz)}

    sides = (-3, -2, -1, 1, 2, 3)
    vw, mw, raw_v, r2_buf = (vw_0, vw_1), (mw_0, mw_1), (raw_0, raw_1), (r2_0, r2_1)

    def load(src, dst, slot):
        copy = pltpu.make_async_copy(src, dst, local_sem.at[slot])
        copy.start()
        return copy

    c_order = load(order, ord_v, 0)
    c_signal = load(signal, sig_v, 1)
    c_dt = load(device_transfer, dt_v, 2)
    c_bt = load(block_transfer, bt_v, 3)
    c_basis = load(leaf_basis, basis_v, 4)
    c_lt = load(leaf_transfer, lt_v, 5)
    c_dc = load(device_coupling, dc_v, 6)
    c_bc = load(block_coupling, bc_v, 7)
    c_tc = load(top_coupling, tc_v, 8)
    c_tiles = load(near_tiles, tiles_v, 9)
    c_lc = load(leaf_coupling, lc_v, 10)

    barrier = pltpu.get_barrier_semaphore()

    @pl.loop(1, n_gz)
    def _(k):
        pl.semaphore_signal(barrier, inc=1, device_id=line_id(k), device_id_type=MESH)

    @pl.loop(1, n_blocks)
    def _(k):
        pl.semaphore_signal(barrier, inc=1, device_id=plane_id(k), device_id_type=MESH)

    for s in sides:
        pl.semaphore_signal(
            barrier, inc=1, device_id=mesh_id(device + s), device_id_type=MESH
        )

    c_dt.wait()
    c_bt.wait()
    own_dt = dt_v[0]
    own_bt = bt_v[0]
    up = placed(rank, 4 * rank, 0) + nn(own_bt, placed(rank, 4 * rank, rank).astype(BF16))
    e1 = parts_of(nn(own_dt, up.astype(BF16)) + placed(rank, 4 * rank, 3 * rank))

    c_order.wait()
    c_signal.wait()
    sig_rows = jnp.concatenate(
        [sig_v[:, q * leaf : (q + 1) * leaf].astype(BF16) for q in range(slabs)], axis=0
    )
    lane_rows = lax.broadcasted_iota(jnp.int32, (leaf, leaf), 0)
    c_basis.wait()
    c_lt.wait()

    upper_lanes = lax.broadcasted_iota(jnp.int32, (rhs, 2 * rank), 1) >= rank

    def twofold(x):
        return jnp.concatenate([x, x], axis=0)

    def moments_of(value, l):
        both = nt(value, twofold(basis_v[l]))
        top = both.astype(BF16).astype(F32)
        return jnp.where(upper_lanes, both - top, top).astype(BF16)

    own = jnp.zeros((rhs, rank), F32)
    for j in range(leaves):
        cols = slice(j * leaf, (j + 1) * leaf)
        spot = ord_v[:, cols]
        low = lax.rem(spot, leaf)
        high = spot // leaf
        hot = jnp.where(lane_rows == low, 1.0, 0.0).astype(BF16)
        hot_v[:, cols] = hot
        picked = nn(sig_rows, hot)
        value = jnp.zeros((rhs, leaf), F32)
        for q in range(slabs):
            value = value + jnp.where(high == q, picked[q * rhs : (q + 1) * rhs], 0.0)
        value = value.astype(BF16)
        vw[0][NEAR_REACH + j] = value
        moment = moments_of(value, j)
        mw[0][LINK_REACH + j] = moment
        own = own + nn(moment, twofold(lt_v[j]))
    msg = full(own, *e1)

    pl.semaphore_wait(barrier, (n_gz - 1) + (n_blocks - 1) + len(sides))

    def r1_copy(a, k):
        return pltpu.make_async_remote_copy(
            src_ref=r1_src.at[a],
            dst_ref=r1_buf.at[a, k],
            send_sem=r1_send.at[a, k],
            recv_sem=r1_recv.at[a, k],
            device_id=line_id(k),
            device_id_type=MESH,
        )

    def r2_copy(a, k):
        return pltpu.make_async_remote_copy(
            src_ref=r2_buf[a].at[block],
            dst_ref=r2_buf[a].at[block],
            send_sem=r2_send.at[a, k],
            recv_sem=r2_recv.at[a, k],
            device_id=plane_id(k),
            device_id_type=MESH,
        )

    def raw_copy(a, n):
        s = sides[n]
        return pltpu.make_async_remote_copy(
            src_ref=raw_v[a].at[DEVICE_REACH],
            dst_ref=raw_v[a].at[DEVICE_REACH - s],
            send_sem=raw_send.at[a, n],
            recv_sem=raw_recv.at[a, n],
            device_id=mesh_id(device + s),
            device_id_type=MESH,
        )

    def halo_copy(a, n):
        ref, reach = (vw, NEAR_REACH) if n < 2 else (mw, LINK_REACH)
        if n % 2 == 0:
            src, dst, s = leaves, 0, 1
        else:
            src, dst, s = reach, reach + leaves, -1
        return pltpu.make_async_remote_copy(
            src_ref=ref[a].at[pl.ds(src, reach)],
            dst_ref=ref[a].at[pl.ds(dst, reach)],
            send_sem=halo_send.at[a, n],
            recv_sem=halo_recv.at[a, n],
            device_id=mesh_id(device + s),
            device_id_type=MESH,
        )

    def send_up(a, message):
        r1_src[a] = message[:, 0 : 2 * rank].astype(BF16)
        raw_v[a][DEVICE_REACH] = message[:, 2 * rank : 4 * rank]

        @pl.loop(1, n_gz)
        def _(k):
            r1_copy(a, k).start()

        for n in range(len(sides)):
            raw_copy(a, n).start()

    def send_across(a):
        @pl.loop(1, n_gz)
        def _(k):
            r1_copy(a, k).wait_recv()

        total = r1_src[a].astype(F32)
        for k in range(1, n_gz):
            total = total + r1_buf[a, k].astype(F32)
        r2_buf[a][block] = total.astype(BF16)

        @pl.loop(1, n_blocks)
        def _(k):
            r2_copy(a, k).start()

    def wait_across(a):
        @pl.loop(1, n_blocks)
        def _(k):
            r2_copy(a, k).wait_recv()

    def far_part(a):
        parts = [r2_buf[a][block_links[0, k]].astype(BF16) for k in range(LINKS)]
        for k in range(LINKS):
            total = jnp.zeros((rhs, 2 * rank), F32)
            for i in range(n_gy):
                total = total + r2_buf[a][top_links[0, k] * n_gy + i].astype(F32)
            parts.append(total.astype(BF16))
        rows = jnp.concatenate(parts, axis=1)
        start = LINKS * 2 * rank
        return nn(rows, mix_v[0, start:]) + nn(rows, mix_v[1, start:])

    def side_part(a):
        for n in range(len(sides)):
            raw_copy(a, n).wait_recv()
        parts = [
            raw_v[a][within(device_links[0, k] - device + DEVICE_REACH, raw_v[a])]
            for k in range(LINKS)
        ]
        end = LINKS * 2 * rank
        return full(jnp.concatenate(parts, axis=1), mix_v[0, :end], mix_v[1, :end])

    def field_of(message):
        field = message[:, 2 * rank : 3 * rank]
        return halves(jnp.concatenate([field, field], axis=1))

    def twice_rows(both):
        return both[0:rhs] + both[rhs:]

    def send_halos(a):
        for n in range(4):
            halo_copy(a, n).start()

    def wait_halos(a):
        for n in range(4):
            halo_copy(a, n).wait_recv()

    def near_and_leaf(a):
        diagonal = lax.broadcasted_iota(jnp.int32, (rhs, LINKS * rank), 1) // rank
        for l in range(leaves):
            total = nn(vw[a][NEAR_REACH + l], tiles_v[l, 0])
            for k in range(1, near_list.shape[0]):
                spot = within(near_list[k, l] - first_leaf + NEAR_REACH, vw[a])
                total = total + nn(vw[a][spot], tiles_v[l, k])
            near_v[l] = total
            stacked = jnp.concatenate(
                [
                    mw[a][within(leaf_links[k, l] - first_leaf + LINK_REACH, mw[a])]
                    for k in range(LINKS)
                ],
                axis=0,
            )
            wide = nn(stacked, twofold(lc_v[l]))
            kept = wide[0:rhs]
            for k in range(1, LINKS):
                kept = jnp.where(diagonal == k, wide[k * rhs : (k + 1) * rhs], kept)
            coup_v[l * 2 * rhs : (l + 1) * 2 * rhs, :] = halves(kept)
        fold = placed(LINKS * rank, rank, 0)
        for k in range(1, LINKS):
            fold = fold + placed(LINKS * rank, rank, -k * rank)
        field = nn(coup_v[...], fold.astype(BF16))
        for l in range(leaves):
            base = l * 2 * rhs
            whole = field[base : base + rhs] + field[base + rhs : base + 2 * rhs]
            near_v[l] = near_v[l] + fine(nn, whole, basis_v[l])

    def scatter(target):
        for j in range(leaves):
            cols = slice(j * leaf, (j + 1) * leaf)
            value = near_v[j]
            top = value.astype(BF16).astype(F32)
            rest = value - top
            high = ord_v[:, cols] // leaf
            for q in range(slabs):
                here = high == q
                rows = slice(q * rhs, (q + 1) * rhs)
                scat_v[rows, cols] = jnp.where(here, top, 0.0).astype(BF16)
                rows = slice((slabs + q) * rhs, (slabs + q + 1) * rhs)
                scat_v[rows, cols] = jnp.where(here, rest, 0.0).astype(BF16)
        done = nt(scat_v[...], hot_v[...])
        done = done[: slabs * rhs] + done[slabs * rhs :]
        for q in range(slabs):
            target[:, q * leaf : (q + 1) * leaf] = done[q * rhs : (q + 1) * rhs]

    send_up(0, msg)
    send_halos(0)

    c_dc.wait()
    c_bc.wait()
    c_tc.wait()
    eye = placed(rank, rank, 0).astype(BF16)
    square = jnp.zeros((rank, rank), F32)
    for l in range(leaves):
        turned = nt(eye, lt_v[l]).astype(BF16)
        qt = halves(nn(turned, basis_v[l]))
        qt_v[l] = qt
        square = square + nt(qt[0:rank], qt[0:rank])
    e2 = parts_of(full(square, *e1) + placed(rank, 4 * rank, 2 * rank))
    picks = [placed(LINKS * rank, rank, -k * rank).astype(BF16) for k in range(LINKS)]
    sides_in = [nn(dc_v[0], pick) for pick in picks]
    blocks_in = [nt(nn(bc_v[0], pick).astype(BF16), own_dt) for pick in picks]
    tops_in = [
        fine(nt, nt(nn(tc_v[0], pick).astype(BF16), own_bt), own_dt) for pick in picks
    ]
    mixed = full(jnp.concatenate(sides_in + blocks_in + tops_in, axis=0), *e2)
    mix_v[...] = jnp.zeros_like(mix_v)
    for n in range(3 * LINKS):
        base = n * 2 * rank + (0 if LINKS <= n < 2 * LINKS else rank)
        for half, value in enumerate(parts_of(mixed[n * rank : (n + 1) * rank])):
            mix_v[half, base : base + rank, :] = value

    send_across(0)

    c_tiles.wait()
    c_lc.wait()
    wait_halos(0)
    near_and_leaf(0)
    local = jnp.zeros((rhs, rank), F32)
    for l in range(leaves):
        local = local + nt(near_v[l].astype(BF16), qt_v[l, 0:rank])
    partial = full(local, *e1) + side_part(0)

    wait_across(0)
    msg = partial + far_part(0)
    send_up(1, msg)

    field = field_of(msg)
    for l in range(leaves):
        value = near_v[l] + twice_rows(nn(field, qt_v[l]))
        near_v[l] = value
        value = value.astype(BF16)
        vw[1][NEAR_REACH + l] = value
        mw[1][LINK_REACH + l] = moments_of(value, l)
    send_halos(1)
    scatter(smoothed)
    send_across(1)
    wait_halos(1)
    near_and_leaf(1)
    partial = side_part(1)
    wait_across(1)
    msg = partial + far_part(1)
    field = field_of(msg)
    for l in range(leaves):
        near_v[l] = near_v[l] + twice_rows(nn(field, qt_v[l]))
    scatter(twice)

    for a in range(2):

        @pl.loop(1, n_gz)
        def _(k):
            r1_copy(a, k).wait_send()

        @pl.loop(1, n_blocks)
        def _(k):
            r2_copy(a, k).wait_send()

        for n in range(len(sides)):
            raw_copy(a, n).wait_send()
        for n in range(4):
            halo_copy(a, n).wait_send()


def solution(mesh):
    sizes = mesh.shape["gx"], mesh.shape["gy"], mesh.shape["gz"]
    n_gx, n_gy, n_gz = sizes

    def shards(
        signal,
        order,
        near_tiles,
        near_list,
        leaf_basis,
        leaf_transfer,
        leaf_coupling,
        leaf_links,
        device_transfer,
        device_coupling,
        device_links,
        block_transfer,
        block_coupling,
        block_links,
        top_coupling,
        top_links,
    ):
        rhs, points = signal.shape
        leaves, rank, leaf = leaf_basis.shape
        n_blocks = n_gx * n_gy
        vmem, far = pltpu.VMEM, pl.BlockSpec(memory_space=pltpu.HBM)
        smem = pl.BlockSpec(memory_space=pltpu.SMEM)
        wide = 2 * rank
        dma = pltpu.SemaphoreType.DMA
        scratch = [
            vmem((rhs, points), F32),
            vmem((1, points), jnp.int32),
            vmem(near_tiles.shape, BF16),
            vmem(leaf_basis.shape, BF16),
            vmem(leaf_transfer.shape, BF16),
            vmem(leaf_coupling.shape, BF16),
            vmem(device_transfer.shape, BF16),
            vmem(device_coupling.shape, BF16),
            vmem(block_transfer.shape, BF16),
            vmem(block_coupling.shape, BF16),
            vmem(top_coupling.shape, BF16),
            vmem((leaf, points), BF16),
            vmem((2 * rhs * points // leaf, points), BF16),
            vmem((leaves + 2 * NEAR_REACH, rhs, leaf), BF16),
            vmem((leaves + 2 * NEAR_REACH, rhs, leaf), BF16),
            vmem((leaves + 2 * LINK_REACH, rhs, wide), BF16),
            vmem((leaves + 2 * LINK_REACH, rhs, wide), BF16),
            vmem((2 * DEVICE_REACH + 1, rhs, wide), F32),
            vmem((2 * DEVICE_REACH + 1, rhs, wide), F32),
            vmem((2, rhs, wide), BF16),
            vmem((2, n_gz, rhs, wide), BF16),
            vmem((n_blocks, rhs, wide), BF16),
            vmem((n_blocks, rhs, wide), BF16),
            vmem((leaves, rhs, leaf), F32),
            vmem((2 * leaves * rhs, LINKS * rank), BF16),
            vmem((leaves, 2 * rank, leaf), BF16),
            vmem((2, 3 * LINKS * wide, 4 * rank), BF16),
            dma((11,)),
            dma((2, 4)),
            dma((2, 4)),
            dma((2, 6)),
            dma((2, 6)),
            dma((2, n_gz)),
            dma((2, n_gz)),
            dma((2, n_blocks)),
            dma((2, n_blocks)),
        ]
        out = jax.ShapeDtypeStruct((rhs, points), F32)
        return pl.pallas_call(
            functools.partial(kernel, n_gx, n_gy, n_gz),
            out_shape=(out, out),
            in_specs=[smem] * 5 + [far] * 11,
            out_specs=(pl.BlockSpec(memory_space=vmem),) * 2,
            scratch_shapes=scratch,
            compiler_params=pltpu.CompilerParams(
                collective_id=0, has_side_effects=True, vmem_limit_bytes=60 * 1024 * 1024
            ),
        )(
            near_list.T,
            leaf_links.T,
            device_links,
            block_links,
            top_links,
            signal,
            order.reshape(1, points),
            near_tiles,
            leaf_basis,
            leaf_transfer,
            leaf_coupling,
            device_transfer,
            device_coupling,
            block_transfer,
            block_coupling,
            top_coupling,
        )

    every = ("gx", "gy", "gz")
    in_specs = (
        P(None, every),
        P(every),
        P(every, None, None, None),
        P(every, None),
        P(every, None, None),
        P(every, None, None),
        P(every, None, None),
        P(every, None),
        P(every, None, None),
        P(every, None, None),
        P(every, None),
        P(("gx", "gy"), None, None),
        P(("gx", "gy"), None, None),
        P(("gx", "gy"), None),
        P("gx", None, None),
        P("gx", None),
    )
    out_specs = (P(None, every), P(None, every))
    return jax.shard_map(
        shards, mesh=mesh, in_specs=in_specs, out_specs=out_specs, check_vma=False
    )
```

time: 244 us -> 44.1 us (0.18)
  the two profiles are of different devices: /device:TPU:32 before, /device:TPU:1 now
where the time goes in v1:
time: 44.1 us; the launch traced here: 43.9 us
  Pallas kernels  39.9 us (90%)
  local copies, waits for them, and re-layouts  3.34 us (8%)
  between operations  0.65 us (1%)
    pallas_call x1, Pallas kernels, shards(): pl.pallas_call(functools.partial(kernel, n_gx, n_gy, n_gz), out_shape=(ou...  39.9 us
    unnamed x2, local copies, waits for them, and re-layouts  3.34 us

profile of v1, /device:TPU:1, one launch (start us, length us, event | category | flops | bytes accessed | tf_op | source)
XLA Modules:
  0.0 43.9 jit_solution(7861668282530569655)
XLA Ops:
  0.6 39.9 %shard_map.167 = (f32[16,4096]{1,0:T(8,128)}, f32[16,4096]{1,0:T(8,128)}) custom-call(s32[3,16]{1,0:T(4,128)} %bitcast.4, s32[3,16]{1,0:T(4,128)} %bitcast.5, s32[1,3]{1,0:T(1,128)} %device_links.1, s32[1,3]{1,0:T(1,128)} %block_links.1, s32[1,3]{1,0:T(1,128)} %top_links.1, f32[16,4096]{1,0:T(8,128)} %signal.1, s32[1,4096]{1,0:T(1,128)} %bitcast.3, ...), custom_call_target="tpu_custom_call" | custom-call | tf_op jit(solution)/shard_map/pallas_call | solution.py:525
  40.6 1.7 %copy.20 = f32[16,4096]{1,0:T(8,128)} copy(f32[16,4096]{1,0:T(8,128)} %get-tuple-element.4) | data formatting | bytes 524288
  42.2 1.7 %copy.21 = f32[16,4096]{1,0:T(8,128)} copy(f32[16,4096]{1,0:T(8,128)} %get-tuple-element.5) | data formatting | bytes 524288

commit v2 on v1

--- a/solution.py
+++ b/solution.py
@@ -103,7 +103,9 @@
     coup_v,
     qt_v,
     mix_v,
+    out_v,
     local_sem,
+    out_sem,
     halo_send,
     halo_recv,
     raw_send,
@@ -116,6 +118,8 @@
     rhs, points = sig_v.shape
     leaves, rank, leaf = basis_v.shape
     slabs = points // leaf
+    shift = leaf.bit_length() - 1
+    assert 1 << shift == leaf
     n_blocks = n_gx * n_gy
     n_devices = n_blocks * n_gz
     gx, gy, gz = lax.axis_index("gx"), lax.axis_index("gy"), lax.axis_index("gz")
@@ -123,17 +127,34 @@
     device = block * n_gz + gz
     first_leaf = device * leaves
 
-    def mesh_id(index):
-        index = lax.rem(index + n_devices, n_devices)
-        row = index // n_gz
-        return {"gx": row // n_gy, "gy": lax.rem(row, n_gy), "gz": lax.rem(index, n_gz)}
+    def wrapped(index, size):
+        index = jnp.where(index >= size, index - size, index)
+        return jnp.where(index < 0, index + size, index)
+
+    def mesh_id(shift):
+        z = gz + shift
+        carry = (z >= n_gz).astype(jnp.int32) - (z < 0).astype(jnp.int32)
+        y = gy + carry
+        carry = (y >= n_gy).astype(jnp.int32) - (y < 0).astype(jnp.int32)
+        return {
+            "gx": wrapped(gx + carry, n_gx),
+            "gy": wrapped(y, n_gy),
+            "gz": wrapped(z, n_gz),
+        }
+
+    def far_first(size):
+        return sorted(range(size), key=lambda step: -min(step, size - step))
+
+    plane = [(x, y) for x in far_first(n_gx) for y in far_first(n_gy) if x or y]
 
     def plane_id(k):
-        other = lax.rem(block + k, n_blocks)
-        return {"gx": other // n_gy, "gy": lax.rem(other, n_gy), "gz": gz}
+        x, y = plane[k]
+        return {"gx": wrapped(gx + x, n_gx), "gy": wrapped(gy + y, n_gy), "gz": gz}
+
+    line = [step for step in far_first(n_gz) if step]
 
     def line_id(k):
-        return {"gx": gx, "gy": gy, "gz": lax.rem(gz + k, n_gz)}
+        return {"gx": gx, "gy": gy, "gz": wrapped(gz + line[k], n_gz)}
 
     sides = (-3, -2, -1, 1, 2, 3)
     vw, mw, raw_v, r2_buf = (vw_0, vw_1), (mw_0, mw_1), (raw_0, raw_1), (r2_0, r2_1)
@@ -157,18 +178,10 @@
 
     barrier = pltpu.get_barrier_semaphore()
 
-    @pl.loop(1, n_gz)
-    def _(k):
-        pl.semaphore_signal(barrier, inc=1, device_id=line_id(k), device_id_type=MESH)
-
-    @pl.loop(1, n_blocks)
-    def _(k):
-        pl.semaphore_signal(barrier, inc=1, device_id=plane_id(k), device_id_type=MESH)
-
-    for s in sides:
-        pl.semaphore_signal(
-            barrier, inc=1, device_id=mesh_id(device + s), device_id_type=MESH
-        )
+    peers = [plane_id(k) for k in range(len(plane))]
+    peers = peers + [line_id(k) for k in range(len(line))] + [mesh_id(s) for s in sides]
+    for peer in peers:
+        pl.semaphore_signal(barrier, inc=1, device_id=peer, device_id_type=MESH)
 
     c_dt.wait()
     c_bt.wait()
@@ -182,7 +195,11 @@
     sig_rows = jnp.concatenate(
         [sig_v[:, q * leaf : (q + 1) * leaf].astype(BF16) for q in range(slabs)], axis=0
     )
-    lane_rows = lax.broadcasted_iota(jnp.int32, (leaf, leaf), 0)
+    def narrow(x):
+        return x.astype(F32).astype(BF16)
+
+    one, zero = jnp.ones((), BF16), jnp.zeros((), BF16)
+    lane_rows = narrow(lax.broadcasted_iota(jnp.int32, (leaf, leaf), 0))
     c_basis.wait()
     c_lt.wait()
 
@@ -200,9 +217,9 @@
     for j in range(leaves):
         cols = slice(j * leaf, (j + 1) * leaf)
         spot = ord_v[:, cols]
-        low = lax.rem(spot, leaf)
-        high = spot // leaf
-        hot = jnp.where(lane_rows == low, 1.0, 0.0).astype(BF16)
+        low = spot & (leaf - 1)
+        high = lax.shift_right_logical(spot, shift)
+        hot = jnp.where(lane_rows == narrow(low), one, zero)
         hot_v[:, cols] = hot
         picked = nn(sig_rows, hot)
         value = jnp.zeros((rhs, leaf), F32)
@@ -215,7 +232,7 @@
         own = own + nn(moment, twofold(lt_v[j]))
     msg = full(own, *e1)
 
-    pl.semaphore_wait(barrier, (n_gz - 1) + (n_blocks - 1) + len(sides))
+    pl.semaphore_wait(barrier, len(peers))
 
     def r1_copy(a, k):
         return pltpu.make_async_remote_copy(
@@ -244,7 +261,7 @@
             dst_ref=raw_v[a].at[DEVICE_REACH - s],
             send_sem=raw_send.at[a, n],
             recv_sem=raw_recv.at[a, n],
-            device_id=mesh_id(device + s),
+            device_id=mesh_id(s),
             device_id_type=MESH,
         )
 
@@ -259,7 +276,7 @@
             dst_ref=ref[a].at[pl.ds(dst, reach)],
             send_sem=halo_send.at[a, n],
             recv_sem=halo_recv.at[a, n],
-            device_id=mesh_id(device + s),
+            device_id=mesh_id(s),
             device_id_type=MESH,
         )
 
@@ -267,30 +284,23 @@
         r1_src[a] = message[:, 0 : 2 * rank].astype(BF16)
         raw_v[a][DEVICE_REACH] = message[:, 2 * rank : 4 * rank]
 
-        @pl.loop(1, n_gz)
-        def _(k):
+        for k in range(len(line)):
             r1_copy(a, k).start()
-
         for n in range(len(sides)):
             raw_copy(a, n).start()
 
     def send_across(a):
-        @pl.loop(1, n_gz)
-        def _(k):
+        for k in range(len(line)):
             r1_copy(a, k).wait_recv()
-
         total = r1_src[a].astype(F32)
-        for k in range(1, n_gz):
+        for k in range(len(line)):
             total = total + r1_buf[a, k].astype(F32)
         r2_buf[a][block] = total.astype(BF16)
-
-        @pl.loop(1, n_blocks)
-        def _(k):
+        for k in range(len(plane)):
             r2_copy(a, k).start()
 
     def wait_across(a):
-        @pl.loop(1, n_blocks)
-        def _(k):
+        for k in range(len(plane)):
             r2_copy(a, k).wait_recv()
 
     def far_part(a):
@@ -358,30 +368,35 @@
             whole = field[base : base + rhs] + field[base + rhs : base + 2 * rhs]
             near_v[l] = near_v[l] + fine(nn, whole, basis_v[l])
 
-    def scatter(target):
+    def scatter(target, slot):
         for j in range(leaves):
             cols = slice(j * leaf, (j + 1) * leaf)
-            value = near_v[j]
-            top = value.astype(BF16).astype(F32)
-            rest = value - top
-            high = ord_v[:, cols] // leaf
+            high = narrow(lax.shift_right_logical(ord_v[:, cols], shift))
+            value = near_v[j].astype(BF16)
             for q in range(slabs):
-                here = high == q
-                rows = slice(q * rhs, (q + 1) * rhs)
-                scat_v[rows, cols] = jnp.where(here, top, 0.0).astype(BF16)
-                rows = slice((slabs + q) * rhs, (slabs + q + 1) * rhs)
-                scat_v[rows, cols] = jnp.where(here, rest, 0.0).astype(BF16)
+                scat_v[q * rhs : (q + 1) * rhs, cols] = jnp.where(
+                    high == jnp.full((), q, BF16), value, zero
+                )
         done = nt(scat_v[...], hot_v[...])
-        done = done[: slabs * rhs] + done[slabs * rhs :]
         for q in range(slabs):
-            target[:, q * leaf : (q + 1) * leaf] = done[q * rhs : (q + 1) * rhs]
+            out_v[slot, :, q * leaf : (q + 1) * leaf] = done[q * rhs : (q + 1) * rhs]
+        copy = pltpu.make_async_copy(out_v.at[slot], target, out_sem.at[slot])
+        copy.start()
+        return copy
+
+    def wait_sends(a):
+        for k in range(len(line)):
+            r1_copy(a, k).wait_send()
+        for k in range(len(plane)):
+            r2_copy(a, k).wait_send()
+        for n in range(len(sides)):
+            raw_copy(a, n).wait_send()
+        for n in range(4):
+            halo_copy(a, n).wait_send()
 
     send_up(0, msg)
     send_halos(0)
 
-    c_dc.wait()
-    c_bc.wait()
-    c_tc.wait()
     eye = placed(rank, rank, 0).astype(BF16)
     square = jnp.zeros((rank, rank), F32)
     for l in range(leaves):
@@ -389,6 +404,9 @@
         qt = halves(nn(turned, basis_v[l]))
         qt_v[l] = qt
         square = square + nt(qt[0:rank], qt[0:rank])
+    c_dc.wait()
+    c_bc.wait()
+    c_tc.wait()
     e2 = parts_of(full(square, *e1) + placed(rank, 4 * rank, 2 * rank))
     picks = [placed(LINKS * rank, rank, -k * rank).astype(BF16) for k in range(LINKS)]
     sides_in = [nn(dc_v[0], pick) for pick in picks]
@@ -403,6 +421,7 @@
         for half, value in enumerate(parts_of(mixed[n * rank : (n + 1) * rank])):
             mix_v[half, base : base + rank, :] = value
 
+
     send_across(0)
 
     c_tiles.wait()
@@ -426,32 +445,40 @@
         vw[1][NEAR_REACH + l] = value
         mw[1][LINK_REACH + l] = moments_of(value, l)
     send_halos(1)
-    scatter(smoothed)
     send_across(1)
+    c_smoothed = scatter(smoothed, 0)
     wait_halos(1)
     near_and_leaf(1)
     partial = side_part(1)
+    wait_sends(0)
+    wait_sends(1)
     wait_across(1)
     msg = partial + far_part(1)
     field = field_of(msg)
     for l in range(leaves):
         near_v[l] = near_v[l] + twice_rows(nn(field, qt_v[l]))
-    scatter(twice)
-
-    for a in range(2):
-
-        @pl.loop(1, n_gz)
-        def _(k):
-            r1_copy(a, k).wait_send()
-
-        @pl.loop(1, n_blocks)
-        def _(k):
-            r2_copy(a, k).wait_send()
-
-        for n in range(len(sides)):
-            raw_copy(a, n).wait_send()
-        for n in range(4):
-            halo_copy(a, n).wait_send()
+    c_twice = scatter(twice, 1)
+    c_smoothed.wait()
+    c_twice.wait()
+
+
+def publish(first, second, smoothed, twice, held, sems):
+    pairs = ((first, smoothed), (second, twice))
+    loads = [
+        pltpu.make_async_copy(src, held.at[n], sems.at[n])
+        for n, (src, dst) in enumerate(pairs)
+    ]
+    stores = [
+        pltpu.make_async_copy(held.at[n], dst, sems.at[2 + n])
+        for n, (src, dst) in enumerate(pairs)
+    ]
+    for copy in loads:
+        copy.start()
+    for load, store in zip(loads, stores):
+        load.wait()
+        store.start()
+    for copy in stores:
+        copy.wait()
 
 
 def solution(mesh):
@@ -479,7 +506,7 @@
         rhs, points = signal.shape
         leaves, rank, leaf = leaf_basis.shape
         n_blocks = n_gx * n_gy
-        vmem, far = pltpu.VMEM, pl.BlockSpec(memory_space=pltpu.HBM)
+        vmem, far = pltpu.VMEM, pl.BlockSpec(memory_space=pl.ANY)
         smem = pl.BlockSpec(memory_space=pltpu.SMEM)
         wide = 2 * rank
         dma = pltpu.SemaphoreType.DMA
@@ -496,7 +523,7 @@
             vmem(block_coupling.shape, BF16),
             vmem(top_coupling.shape, BF16),
             vmem((leaf, points), BF16),
-            vmem((2 * rhs * points // leaf, points), BF16),
+            vmem((rhs * points // leaf, points), BF16),
             vmem((leaves + 2 * NEAR_REACH, rhs, leaf), BF16),
             vmem((leaves + 2 * NEAR_REACH, rhs, leaf), BF16),
             vmem((leaves + 2 * LINK_REACH, rhs, wide), BF16),
@@ -511,7 +538,9 @@
             vmem((2 * leaves * rhs, LINKS * rank), BF16),
             vmem((leaves, 2 * rank, leaf), BF16),
             vmem((2, 3 * LINKS * wide, 4 * rank), BF16),
+            vmem((2, rhs, points), F32),
             dma((11,)),
+            dma((2,)),
             dma((2, 4)),
             dma((2, 4)),
             dma((2, 6)),
@@ -522,11 +551,11 @@
             dma((2, n_blocks)),
         ]
         out = jax.ShapeDtypeStruct((rhs, points), F32)
-        return pl.pallas_call(
+        results = pl.pallas_call(
             functools.partial(kernel, n_gx, n_gy, n_gz),
             out_shape=(out, out),
             in_specs=[smem] * 5 + [far] * 11,
-            out_specs=(pl.BlockSpec(memory_space=vmem),) * 2,
+            out_specs=(far,) * 2,
             scratch_shapes=scratch,
             compiler_params=pltpu.CompilerParams(
                 collective_id=0, has_side_effects=True, vmem_limit_bytes=60 * 1024 * 1024
@@ -549,6 +578,13 @@
             block_coupling,
             top_coupling,
         )
+        return pl.pallas_call(
+            publish,
+            out_shape=(out, out),
+            in_specs=[far] * 2,
+            out_specs=(far,) * 2,
+            scratch_shapes=[vmem((2, rhs, points), F32), dma((4,))],
+        )(*results)
 
     every = ("gx", "gy", "gz")
     in_specs = (

time: 44.1 us -> 38.5 us (0.87)
  local copies, waits for them, and re-layouts: 3.34 us -> 0 us
  Pallas kernels: 39.9 us -> 37.7 us
    pallas_call x1, Pallas kernels: 39.9 us -> 36 us  [shards(): pl.pallas_call(functools.partial(kernel, n_gx, n_gy, n_gz), out_shape=(ou...]
    unnamed x2 -> x0, local copies, waits for them, and re-layouts: 3.34 us -> none
    pallas_call x0 -> x1, Pallas kernels: none -> 1.77 us  [shards(): pl.pallas_call(publish, out_shape=(out, out), in_specs=[far] * 2, out_spe...]
where the time goes in v2:
time: 38.5 us; the launch traced here: 38.4 us
  Pallas kernels  37.7 us (98%)
  between operations  0.64 us (2%)
    pallas_call x1, Pallas kernels, shards(): pl.pallas_call(functools.partial(kernel, n_gx, n_gy, n_gz), out_shape=(ou...  36 us
    pallas_call x1, Pallas kernels, shards(): pl.pallas_call(publish, out_shape=(out, out), in_specs=[far] * 2, out_spe...  1.77 us

profile of v2, /device:TPU:1, one launch (start us, length us, event | category | flops | bytes accessed | tf_op | source)
XLA Modules:
  0.0 38.4 jit_solution(7793957248078143252)
XLA Ops:
  0.6 36.0 %shard_map.167 = (f32[16,4096]{1,0:T(8,128)}, f32[16,4096]{1,0:T(8,128)}) custom-call(s32[3,16]{1,0:T(4,128)} %bitcast.4, s32[3,16]{1,0:T(4,128)} %bitcast.5, s32[1,3]{1,0:T(1,128)} %device_links.1, s32[1,3]{1,0:T(1,128)} %block_links.1, s32[1,3]{1,0:T(1,128)} %top_links.1, f32[16,4096]{1,0:T(8,128)} %signal.1, s32[1,4096]{1,0:T(1,128)} %bitcast.3, ...), custom_call_target="tpu_custom_call" | custom-call | tf_op jit(solution)/shard_map/pallas_call | solution.py:554
  36.6 1.8 %shard_map.168 = (f32[16,4096]{1,0:T(8,128)}, f32[16,4096]{1,0:T(8,128)}) custom-call(f32[16,4096]{1,0:T(8,128)} %get-tuple-element.4.first, f32[16,4096]{1,0:T(8,128)} %get-tuple-element.5.second), custom_call_target="tpu_custom_call" | custom-call | tf_op jit(solution)/shard_map/pallas_call | solution.py:581

commit v3 on v2

--- a/solution.py
+++ b/solution.py
@@ -58,11 +58,11 @@
     n_gx,
     n_gy,
     n_gz,
-    near_list,
-    leaf_links,
-    device_links,
-    block_links,
-    top_links,
+    near_list_in,
+    leaf_links_in,
+    device_links_in,
+    block_links_in,
+    top_links_in,
     signal,
     order,
     near_tiles,
@@ -76,6 +76,11 @@
     top_coupling,
     smoothed,
     twice,
+    near_list,
+    leaf_links,
+    device_links,
+    block_links,
+    top_links,
     sig_v,
     ord_v,
     tiles_v,
@@ -175,6 +180,13 @@
     c_tc = load(top_coupling, tc_v, 8)
     c_tiles = load(near_tiles, tiles_v, 9)
     c_lc = load(leaf_coupling, lc_v, 10)
+    c_lists = [
+        load(near_list_in, near_list, 11),
+        load(leaf_links_in, leaf_links, 12),
+        load(device_links_in, device_links, 13),
+        load(block_links_in, block_links, 14),
+        load(top_links_in, top_links, 15),
+    ]
 
     barrier = pltpu.get_barrier_semaphore()
 
@@ -183,12 +195,7 @@
     for peer in peers:
         pl.semaphore_signal(barrier, inc=1, device_id=peer, device_id_type=MESH)
 
-    c_dt.wait()
-    c_bt.wait()
-    own_dt = dt_v[0]
-    own_bt = bt_v[0]
-    up = placed(rank, 4 * rank, 0) + nn(own_bt, placed(rank, 4 * rank, rank).astype(BF16))
-    e1 = parts_of(nn(own_dt, up.astype(BF16)) + placed(rank, 4 * rank, 3 * rank))
+    mix_v[...] = jnp.zeros_like(mix_v)
 
     c_order.wait()
     c_signal.wait()
@@ -200,9 +207,6 @@
 
     one, zero = jnp.ones((), BF16), jnp.zeros((), BF16)
     lane_rows = narrow(lax.broadcasted_iota(jnp.int32, (leaf, leaf), 0))
-    c_basis.wait()
-    c_lt.wait()
-
     upper_lanes = lax.broadcasted_iota(jnp.int32, (rhs, 2 * rank), 1) >= rank
 
     def twofold(x):
@@ -213,7 +217,6 @@
         top = both.astype(BF16).astype(F32)
         return jnp.where(upper_lanes, both - top, top).astype(BF16)
 
-    own = jnp.zeros((rhs, rank), F32)
     for j in range(leaves):
         cols = slice(j * leaf, (j + 1) * leaf)
         spot = ord_v[:, cols]
@@ -227,9 +230,21 @@
             value = value + jnp.where(high == q, picked[q * rhs : (q + 1) * rhs], 0.0)
         value = value.astype(BF16)
         vw[0][NEAR_REACH + j] = value
-        moment = moments_of(value, j)
-        mw[0][LINK_REACH + j] = moment
-        own = own + nn(moment, twofold(lt_v[j]))
+    c_basis.wait()
+    c_lt.wait()
+    moments = [moments_of(vw[0][NEAR_REACH + j], j) for j in range(leaves)]
+    for j in range(leaves):
+        mw[0][LINK_REACH + j] = moments[j]
+    weights = [twofold(lt_v[j]) for j in range(leaves)]
+    own = nn(jnp.concatenate(moments, axis=1), jnp.concatenate(weights, axis=0))
+
+    c_dt.wait()
+    c_bt.wait()
+    own_dt = dt_v[0]
+    own_bt = bt_v[0]
+    up = placed(rank, 4 * rank, 0) + nn(own_bt, placed(rank, 4 * rank, rank).astype(BF16))
+    e1 = parts_of(nn(own_dt, up.astype(BF16)) + placed(rank, 4 * rank, 3 * rank))
+
     msg = full(own, *e1)
 
     pl.semaphore_wait(barrier, len(peers))
@@ -238,8 +253,8 @@
         return pltpu.make_async_remote_copy(
             src_ref=r1_src.at[a],
             dst_ref=r1_buf.at[a, k],
-            send_sem=r1_send.at[a, k],
-            recv_sem=r1_recv.at[a, k],
+            send_sem=r1_send.at[a],
+            recv_sem=r1_recv.at[a],
             device_id=line_id(k),
             device_id_type=MESH,
         )
@@ -248,8 +263,8 @@
         return pltpu.make_async_remote_copy(
             src_ref=r2_buf[a].at[block],
             dst_ref=r2_buf[a].at[block],
-            send_sem=r2_send.at[a, k],
-            recv_sem=r2_recv.at[a, k],
+            send_sem=r2_send.at[a],
+            recv_sem=r2_recv.at[a],
             device_id=plane_id(k),
             device_id_type=MESH,
         )
@@ -259,8 +274,8 @@
         return pltpu.make_async_remote_copy(
             src_ref=raw_v[a].at[DEVICE_REACH],
             dst_ref=raw_v[a].at[DEVICE_REACH - s],
-            send_sem=raw_send.at[a, n],
-            recv_sem=raw_recv.at[a, n],
+            send_sem=raw_send.at[a],
+            recv_sem=raw_recv.at[a],
             device_id=mesh_id(s),
             device_id_type=MESH,
         )
@@ -274,11 +289,27 @@
         return pltpu.make_async_remote_copy(
             src_ref=ref[a].at[pl.ds(src, reach)],
             dst_ref=ref[a].at[pl.ds(dst, reach)],
-            send_sem=halo_send.at[a, n],
-            recv_sem=halo_recv.at[a, n],
+            send_sem=halo_send.at[a],
+            recv_sem=halo_recv.at[a],
             device_id=mesh_id(s),
             device_id_type=MESH,
         )
+
+    def group(ref, count, sem):
+        ref = ref.at[pl.ds(0, count)]
+        return pltpu.make_async_copy(ref, ref, sem)
+
+    def r1_all(a, sem):
+        return group(r1_buf.at[a], len(line), sem.at[a])
+
+    def r2_all(a, sem):
+        return group(r2_buf[a], len(plane), sem.at[a])
+
+    def raw_all(a, sem):
+        return group(raw_v[a], len(sides), sem.at[a])
+
+    def halo_all(a, sem):
+        return group(vw[a], 2 * (NEAR_REACH + NEAR_REACH), sem.at[a])
 
     def send_up(a, message):
         r1_src[a] = message[:, 0 : 2 * rank].astype(BF16)
@@ -290,8 +321,7 @@
             raw_copy(a, n).start()
 
     def send_across(a):
-        for k in range(len(line)):
-            r1_copy(a, k).wait_recv()
+        r1_all(a, r1_recv).wait()
         total = r1_src[a].astype(F32)
         for k in range(len(line)):
             total = total + r1_buf[a, k].astype(F32)
@@ -300,8 +330,7 @@
             r2_copy(a, k).start()
 
     def wait_across(a):
-        for k in range(len(plane)):
-            r2_copy(a, k).wait_recv()
+        r2_all(a, r2_recv).wait()
 
     def far_part(a):
         parts = [r2_buf[a][block_links[0, k]].astype(BF16) for k in range(LINKS)]
@@ -315,8 +344,7 @@
         return nn(rows, mix_v[0, start:]) + nn(rows, mix_v[1, start:])
 
     def side_part(a):
-        for n in range(len(sides)):
-            raw_copy(a, n).wait_recv()
+        raw_all(a, raw_recv).wait()
         parts = [
             raw_v[a][within(device_links[0, k] - device + DEVICE_REACH, raw_v[a])]
             for k in range(LINKS)
@@ -336,8 +364,7 @@
             halo_copy(a, n).start()
 
     def wait_halos(a):
-        for n in range(4):
-            halo_copy(a, n).wait_recv()
+        halo_all(a, halo_recv).wait()
 
     def near_and_leaf(a):
         diagonal = lax.broadcasted_iota(jnp.int32, (rhs, LINKS * rank), 1) // rank
@@ -385,18 +412,23 @@
         return copy
 
     def wait_sends(a):
-        for k in range(len(line)):
-            r1_copy(a, k).wait_send()
-        for k in range(len(plane)):
-            r2_copy(a, k).wait_send()
-        for n in range(len(sides)):
-            raw_copy(a, n).wait_send()
-        for n in range(4):
-            halo_copy(a, n).wait_send()
+        r1_all(a, r1_send).wait()
+        r2_all(a, r2_send).wait()
+        raw_all(a, raw_send).wait()
+        halo_all(a, halo_send).wait()
 
     send_up(0, msg)
     send_halos(0)
 
+    c_dc.wait()
+    c_bc.wait()
+    c_tc.wait()
+    picks = [placed(LINKS * rank, rank, -k * rank).astype(BF16) for k in range(LINKS)]
+    sides_in = [nn(dc_v[0], pick) for pick in picks]
+    blocks_in = [nt(nn(bc_v[0], pick).astype(BF16), own_dt) for pick in picks]
+    tops_in = [
+        fine(nt, nt(nn(tc_v[0], pick).astype(BF16), own_bt), own_dt) for pick in picks
+    ]
     eye = placed(rank, rank, 0).astype(BF16)
     square = jnp.zeros((rank, rank), F32)
     for l in range(leaves):
@@ -404,18 +436,8 @@
         qt = halves(nn(turned, basis_v[l]))
         qt_v[l] = qt
         square = square + nt(qt[0:rank], qt[0:rank])
-    c_dc.wait()
-    c_bc.wait()
-    c_tc.wait()
     e2 = parts_of(full(square, *e1) + placed(rank, 4 * rank, 2 * rank))
-    picks = [placed(LINKS * rank, rank, -k * rank).astype(BF16) for k in range(LINKS)]
-    sides_in = [nn(dc_v[0], pick) for pick in picks]
-    blocks_in = [nt(nn(bc_v[0], pick).astype(BF16), own_dt) for pick in picks]
-    tops_in = [
-        fine(nt, nt(nn(tc_v[0], pick).astype(BF16), own_bt), own_dt) for pick in picks
-    ]
     mixed = full(jnp.concatenate(sides_in + blocks_in + tops_in, axis=0), *e2)
-    mix_v[...] = jnp.zeros_like(mix_v)
     for n in range(3 * LINKS):
         base = n * 2 * rank + (0 if LINKS <= n < 2 * LINKS else rank)
         for half, value in enumerate(parts_of(mixed[n * rank : (n + 1) * rank])):
@@ -424,6 +446,8 @@
 
     send_across(0)
 
+    for copy in c_lists:
+        copy.wait()
     c_tiles.wait()
     c_lc.wait()
     wait_halos(0)
@@ -507,10 +531,10 @@
         leaves, rank, leaf = leaf_basis.shape
         n_blocks = n_gx * n_gy
         vmem, far = pltpu.VMEM, pl.BlockSpec(memory_space=pl.ANY)
-        smem = pl.BlockSpec(memory_space=pltpu.SMEM)
         wide = 2 * rank
         dma = pltpu.SemaphoreType.DMA
-        scratch = [
+        lists = (near_list.T, leaf_links.T, device_links, block_links, top_links)
+        scratch = [pltpu.SMEM(x.shape, jnp.int32) for x in lists] + [
             vmem((rhs, points), F32),
             vmem((1, points), jnp.int32),
             vmem(near_tiles.shape, BF16),
@@ -539,33 +563,29 @@
             vmem((leaves, 2 * rank, leaf), BF16),
             vmem((2, 3 * LINKS * wide, 4 * rank), BF16),
             vmem((2, rhs, points), F32),
-            dma((11,)),
-            dma((2,)),
-            dma((2, 4)),
-            dma((2, 4)),
-            dma((2, 6)),
-            dma((2, 6)),
-            dma((2, n_gz)),
-            dma((2, n_gz)),
-            dma((2, n_blocks)),
-            dma((2, n_blocks)),
+            dma((16,)),
+            dma((2,)),
+            dma((2,)),
+            dma((2,)),
+            dma((2,)),
+            dma((2,)),
+            dma((2,)),
+            dma((2,)),
+            dma((2,)),
+            dma((2,)),
         ]
         out = jax.ShapeDtypeStruct((rhs, points), F32)
         results = pl.pallas_call(
             functools.partial(kernel, n_gx, n_gy, n_gz),
             out_shape=(out, out),
-            in_specs=[smem] * 5 + [far] * 11,
+            in_specs=[far] * 16,
             out_specs=(far,) * 2,
             scratch_shapes=scratch,
             compiler_params=pltpu.CompilerParams(
                 collective_id=0, has_side_effects=True, vmem_limit_bytes=60 * 1024 * 1024
             ),
         )(
-            near_list.T,
-            leaf_links.T,
-            device_links,
-            block_links,
-            top_links,
+            *lists,
             signal,
             order.reshape(1, points),
             near_tiles,

time: 38.5 us -> 35.9 us (0.932)
  Pallas kernels: 37.7 us -> 35.1 us
    pallas_call x1, Pallas kernels: 36 us -> 33.3 us  [shards(): pl.pallas_call(functools.partial(kernel, n_gx, n_gy, n_gz), out_shape=(ou...]
where the time goes in v3:
time: 35.9 us; the launch traced here: 35.8 us
  Pallas kernels  35.1 us (98%)
  between operations  0.64 us (2%)
    pallas_call x1, Pallas kernels, shards(): pl.pallas_call(functools.partial(kernel, n_gx, n_gy, n_gz), out_shape=(ou...  33.3 us
    pallas_call x1, Pallas kernels, shards(): pl.pallas_call(publish, out_shape=(out, out), in_specs=[far] * 2, out_spe...  1.77 us

profile of v3, /device:TPU:1, one launch (start us, length us, event | category | flops | bytes accessed | tf_op | source)
XLA Modules:
  0.0 35.8 jit_solution(15654448136600654871)
XLA Ops:
  0.6 33.3 %shard_map.167 = (f32[16,4096]{1,0:T(8,128)}, f32[16,4096]{1,0:T(8,128)}) custom-call(s32[3,16]{1,0:T(4,128)} %bitcast.4, s32[3,16]{1,0:T(4,128)} %bitcast.5, s32[1,3]{1,0:T(1,128)} %device_links_in.1, s32[1,3]{1,0:T(1,128)} %block_links_in.1, s32[1,3]{1,0:T(1,128)} %top_links_in.1, f32[16,4096]{1,0:T(8,128)} %signal.1, s32[1,4096]{1,0:T(1,128)} %bitcast.3, ...), custom_call_target="tpu_custom_call" | custom-call | tf_op jit(solution)/shard_map/pallas_call | solution.py:578
  34.0 1.8 %shard_map.168 = (f32[16,4096]{1,0:T(8,128)}, f32[16,4096]{1,0:T(8,128)}) custom-call(f32[16,4096]{1,0:T(8,128)} %get-tuple-element.4.first, f32[16,4096]{1,0:T(8,128)} %get-tuple-element.5.second), custom_call_target="tpu_custom_call" | custom-call | tf_op jit(solution)/shard_map/pallas_call | solution.py:601
